TPU v7x, 512 devices: a whole 4x8x8 slice. The times are simulated.
512 devices in a mesh: frames: 128 (over x, y_hi, z), heads: 4 (over y_lo, core).
Axes of the slice: x: 4, y: 8 (y_hi: 4, y_lo: 2; y = y_hi * 2 + y_lo), z: 8, core: 2. Of those that a mesh axis runs over, the one named last changes fastest.
Arguments:
- queries: bfloat16 [16384, 4096], P('frames', 'heads'), may hold values from -9 to 9
- keys: bfloat16 [16384, 512], P(('frames', 'heads')), may hold values from -4.5 to 4.5
- values: bfloat16 [16384, 512], P(('frames', 'heads')), may hold values from -6 to 6
- block_mask: int32 [128, 128], replicated, may hold values from 0 to 1, as said below
- lengths: int32 [128], replicated, may hold values from 64 to 128, as said below
Outputs:
- attended: bfloat16 [16384, 4096], P('frames', 'heads')
Inputs may be any that keep to these rules, and one draw needn't show every extreme that they name: block_mask[i, i] = 1 and block_mask[i, j] = 0 for j > i. `lengths`: some frame group is full in every draw.
All inputs are finite; a program needn't handle non-finite values.
Results may differ from a plain program's by a relative error of at most 0.0055.
Values may be sent and summed in bfloat16 or wider, within the bound.
No kernel may reach another device: no remote copies, remote signals or barrier semaphores. Data moves between devices by JAX's collectives and lax.ppermute only.
A program may use at most 64 MiB of HBM per device.

v0:
```python
import math

import jax
import jax.numpy as jnp
from jax import lax
from jax.sharding import PartitionSpec as P

HEAD_DIM = 128


masked_score = -1e30


def side_by_side(arrays, axis, dim, along):
    both = jnp.concatenate(arrays, axis=along)
    result, at, gathered = (lax.all_gather(both, axis, axis=dim, tiled=True), 0, [])
    for a in arrays:
        gathered.append(lax.slice_in_dim(result, at, at + a.shape[along], axis=along))
        at += a.shape[along]
    return tuple(gathered)


def attend(query_sets, keys_mine, values_mine, block_mask, lengths, group_tokens):
    kv_local = keys_mine.shape[1] // HEAD_DIM
    q_local = query_sets[0][0].shape[1] // HEAD_DIM
    per_kv = q_local // kv_local
    scale = HEAD_DIM ** (-0.5)
    group_count = block_mask.shape[0]
    group_ids = jnp.arange(group_count, dtype=jnp.int32)
    prepared = []
    initial = []
    for rows, owner in query_sets:
        count = rows.shape[0]
        prepared.append(
            (
                rows.reshape(count, kv_local, per_kv, HEAD_DIM),
                lax.dynamic_slice_in_dim(block_mask, owner, 1, 0)[0],
            )
        )
        initial.append(
            (
                jnp.full((kv_local, per_kv, count), masked_score, jnp.float32),
                jnp.zeros((kv_local, per_kv, count), jnp.float32),
                jnp.zeros((count, kv_local, per_kv, HEAD_DIM), jnp.float32),
            )
        )
    key_piece, value_piece = side_by_side((keys_mine, values_mine), "frames", 0, 1)
    fold_rows = key_piece.shape[0]
    width = math.gcd(fold_rows, 512)
    blocks = fold_rows // width
    key_blocks = key_piece.reshape(blocks, width, kv_local, HEAD_DIM)
    value_blocks = value_piece.reshape(blocks, width, kv_local, HEAD_DIM)

    def one_block(state, inputs):
        key_block, value_block, number = inputs
        positions = number * width + jnp.arange(width, dtype=jnp.int32)
        key_group = positions // group_tokens
        within = positions % group_tokens
        onehot = (key_group[:, None] == group_ids[None, :]).astype(jnp.int32)
        live_len = jnp.sum(onehot * lengths[None, :], axis=1)
        updated = []
        for (query_rows, mask_row), (running_max, running_total, running_acc) in zip(
            prepared, state
        ):
            allowed = jnp.sum(onehot * mask_row[None, :], axis=1)
            valid = (allowed > 0) & (within < live_len)

            def update(current):
                old_max, old_total, old_acc = current
                scores = (
                    jnp.einsum(
                        "tkgd,skd->kgts", query_rows, key_block, preferred_element_type=jnp.float32
                    )
                    * scale
                )
                scores = jnp.where(valid[None, None, None, :], scores, masked_score)
                new_max = jnp.maximum(old_max, jnp.max(scores, axis=-1))
                probs = jnp.exp(scores - new_max[..., None])
                factor = jnp.exp(old_max - new_max)
                new_total = old_total * factor + jnp.sum(probs, axis=-1)
                added = jnp.einsum(
                    "kgts,skd->tkgd",
                    probs.astype(jnp.bfloat16),
                    value_block,
                    preferred_element_type=jnp.float32,
                )
                new_acc = old_acc * jnp.transpose(factor, (2, 0, 1))[..., None] + added
                return (new_max, new_total, new_acc)

            updated.append(
                lax.cond(
                    jnp.any(valid),
                    update,
                    lambda current: current,
                    (running_max, running_total, running_acc),
                )
            )
        return (tuple(updated), None)

    numbers = jnp.arange(blocks, dtype=jnp.int32)
    final, unused = lax.scan(one_block, tuple(initial), (key_blocks, value_blocks, numbers))
    results = []
    for (rows, owner), (running_max, running_total, running_acc) in zip(query_sets, final):
        output = running_acc / jnp.transpose(running_total, (2, 0, 1))[..., None]
        results.append(output.astype(jnp.bfloat16).reshape(rows.shape[0], q_local * HEAD_DIM))
    return results


def local(queries, keys, values, block_mask, lengths):
    keys_mine, values_mine = (
        lax.all_to_all(keys, "heads", split_axis=1, concat_axis=0, tiled=True),
        lax.all_to_all(values, "heads", split_axis=1, concat_axis=0, tiled=True),
    )
    group_tokens = queries.shape[0]
    frame_index = lax.axis_index("frames")
    outputs = attend(
        [(queries, frame_index)], keys_mine, values_mine, block_mask, lengths, group_tokens
    )
    return outputs[0]


def solution(mesh):
    return jax.shard_map(
        local,
        mesh=mesh,
        in_specs=(
            P("frames", "heads"),
            P(("frames", "heads"), None),
            P(("frames", "heads"), None),
            P(),
            P(),
        ),
        out_specs=P("frames", "heads"),
        check_vma=False,
    )
```

profile of v0, /device:TPU:126, one launch (start us, length us, event | category | flops | bytes accessed | tf_op | source)
XLA Modules:
  0.0 406.5 jit_solution(18394463365017490447)
XLA Ops:
  7.9 4.6 %all-to-all-start = ((bf16[32,4,128]{2,0,1:T(8,128)(2,1)}), bf16[32,4,128]{2,0,1:T(8,128)(2,1)S(1)}, u32[]{:S(2)}, u32[]{:S(2)}) async-start(bf16[32,4,128]{2,0,1:T(8,128)(2,1)} %copy_bitcast_fusion.1), calls=%async_computation | async-start | bytes 65536 | tf_op jit(solution)/shard_map/all_to_all | solution.py:111
  14.5 6.3 %all_to_all.38 = bf16[32,4,128]{2,0,1:T(8,128)(2,1)S(1)} all-to-all(bf16[32,4,128]{2,0,1:T(8,128)(2,1)S(1)} %copy_bitcast_fusion), channel_id=1, replica_groups=mesh['frames'=128,'heads'=4] {'heads'}, dimensions={1} | all-to-all | bytes 65536 | tf_op jit(solution)/shard_map/all_to_all | solution.py:112
  22.8 154.0 %all-gather.2.cloned.1.call-done = bf16[16384,256]{1,0:T(8,128)(2,1)} async-done(((bf16[128,256]{1,0:T(8,128)(2,1)}), bf16[16384,256]{1,0:T(8,128)(2,1)}) %all-gather.2.cloned.1.call-update) | async-done | bytes 8388624 | tf_op jit(solution)/shard_map/all_gather | solution.py:16
  176.8 5.7 %fusion.34 = (bf16[16384,128]{1,0:T(8,128)(2,1)}, bf16[16384,128]{1,0:T(8,128)(2,1)}) fusion(bf16[16384,256]{1,0:T(8,128)(2,1)} %all-gather.2.cloned.1.call-done), kind=kLoop, calls=%fused_computation.51 | loop fusion | bytes 16777216 | tf_op jit(solution)/shard_map/slice | solution.py:18
  182.5 6.5 %copy.24 = bf16[32,512,1,128]{1,3,2,0:T(8,128)(2,1)} copy(bf16[32,512,1,128]{3,1,0,2:T(8,128)(2,1)} %bitcast.92) | data formatting | bytes 8388608
  189.1 209.7 %while.17 = (s32[]{:T(128)}, f32[1,8,128]{2,1,0:T(8,128)S(1)}, f32[1,8,128]{2,1,0:T(8,128)S(1)}, f32[128,1,8,128]{0,3,2,1:T(8,128)S(1)}, s32[32]{0:T(128)S(1)}, ...) while((s32[]{:T(128)}, f32[1,8,128]{2,1,0:T(8,128)S(1)}, ...), condition=%wide.region_8.9_spmd.clone, body=%wide.region_0.8_spmd.clone.sunk | while | flops 274810880 | bytes 7946515 | solution.py:101
  192.1 3.7 conditional.3
  198.7 3.7 conditional.3
  205.4 3.7 conditional.3
  212.1 3.7 conditional.3
  218.7 3.7 conditional.3
  225.4 3.7 conditional.3
  238.7 3.7 conditional.3
  252.1 3.7 conditional.3
  265.4 3.7 conditional.3
  278.7 3.7 conditional.3
  292.0 3.7 conditional.3
  305.4 3.7 conditional.3
  318.7 3.7 conditional.3
  332.0 3.7 conditional.3
  345.4 3.7 conditional.3
  358.7 3.7 conditional.3
  372.0 3.7 conditional.3
  385.4 3.7 conditional.3
  (347 shorter events, 217.6 us)
Async XLA Ops:
  6.5 16.2 %copy-start = (s32[128,128]{1,0:T(8,128)S(1)}, s32[128,128]{1,0:T(8,128)}, u32[]{:S(2)}) copy-start(s32[128,128]{1,0:T(8,128)} %param.12) | copy-start | bytes 196612
  7.9 6.5 %all-to-all-start = ((bf16[32,4,128]{2,0,1:T(8,128)(2,1)}), bf16[32,4,128]{2,0,1:T(8,128)(2,1)S(1)}, u32[]{:S(2)}, u32[]{:S(2)}) async-start(bf16[32,4,128]{2,0,1:T(8,128)(2,1)} %copy_bitcast_fusion.1), calls=%async_computation | async-start | bytes 65536 | tf_op jit(solution)/shard_map/all_to_all | solution.py:111
  12.5 164.3 %all-gather.2.cloned.1.call-start = ((), (), s32[]{:S(2)}) async-start(), calls=%async_computation.2 | async-start | bytes 8454144 | tf_op jit(solution)/shard_map/all_gather | solution.py:16
  182.5 6.5 %copy-start.1 = (s32[128]{0:T(128)S(1)}, s32[128]{0:T(128)}, u32[]{:S(2)}) copy-start(s32[128]{0:T(128)} %param.13) | copy-start | bytes 1540
Sparse Core Ops, SparseCore 0:
  21.6 155.2 all-gather.1
where the time goes:
time: 410 us; the launch traced here: 406 us
  waiting for transfers between devices  155 us (38%)
  matrix products  95.8 us (23%)
  other arithmetic  49.8 us (12%)
  loops' own time  45.9 us (11%)
  local copies, waits for them, and re-layouts  35.4 us (9%)
  between operations  13.5 us (3%)
  blocking collectives  6.29 us (2%)
  starting transfers between devices  4.58 us (1%)
    all_gather x1, waiting for transfers between devices, side_by_side(): lax.all_gather(both, axis, axis=dim, tiled=True)  154 us
    dot_general x31, matrix products, update(): jnp.einsum('kgts,skd->tkgd', probs.astype(jnp.bfloat16), value_block, pre...  53.8 us
    another operation x1, loops' own time, attend(): lax.scan(one_block, tuple(initial), (key_blocks, value_blocks, numbers))  44.1 us
    dot_general x31, matrix products, update(): jnp.einsum('tkgd,skd->kgts', query_rows, key_block, preferred_element_typ...  42 us
    reduce_or x32, other arithmetic, one_block(): jnp.any(valid)  23.3 us
    dynamic_slice x32, local copies, waits for them, and re-layouts, attend(): lax.scan(one_block, tuple(initial), (key_blocks, value_blocks, numbers))  18.8 us
    reduce_sum x31, other arithmetic, update(): new_total = old_total * factor + jnp.sum(probs, axis=-1)  15.3 us
    reduce_sum x32, other arithmetic, one_block(): allowed = jnp.sum(onehot * mask_row[None, :], axis=1)  9.65 us
  transfers between devices with their start and end apart: 2, of which 2 were waited for; matrix products, arithmetic and copies ran while one was open for 1% of the time, Pallas kernels for 0%

commit v1 on v0

v1 whole, which is shorter than its diff:
```python
import functools
import math

import jax
import jax.numpy as jnp
from jax import lax
from jax.experimental import pallas as pl
from jax.experimental.pallas import tpu as pltpu
from jax.sharding import Mesh, PartitionSpec as P

D = 128
LOG2E = math.log2(math.e)
NEG = -1e30
NB = 512
TEAM = 4
PART = 32


def attend_kernel(me_ref, mask_ref, len_ref, q_ref, kv_ref, o_ref, kf, vf, acc, mx, sm):
    groups = mask_ref.shape[0]
    per_x = groups // TEAM
    tokens = q_ref.shape[1]
    heads = q_ref.shape[2] // D
    half = heads // 2
    rows = half * tokens
    x, rest = me_ref[0], me_ref[1]
    scale = D**-0.5 * LOG2E

    vf[...] = jnp.zeros_like(vf)

    def one_team(g, _):
        mine = g * per_x + rest

        def pack(c, off):
            j = (c // 4 % 4) * per_x + (c % 4) * 8 + c // 16
            at = pl.multiple_of(c * PART, PART)
            kf[pl.ds(off, PART), :] = kv_ref[pl.ds(at, PART), :D].astype(jnp.float32)
            vf[pl.ds(off, PART), :] = kv_ref[pl.ds(at, PART), D:].astype(jnp.float32)
            live = (len_ref[j] - x + TEAM - 1) // TEAM
            return off + jnp.where(mask_ref[mine, j] > 0, live, 0)

        count = lax.fori_loop(0, groups, pack, jnp.int32(0), unroll=8)

        acc[...] = jnp.zeros_like(acc)
        mx[...] = jnp.full_like(mx, NEG)
        sm[...] = jnp.zeros_like(sm)

        def block(b, _):
            at = pl.multiple_of(b * NB, NB)
            keys = kf[pl.ds(at, NB), :].astype(jnp.bfloat16)
            vals = vf[pl.ds(at, NB), :].astype(jnp.bfloat16)
            live = lax.broadcasted_iota(jnp.int32, (1, NB), 1) < count - at
            for part in range(2):
                r = pl.ds(part * rows, rows)
                q = jnp.concatenate(
                    [q_ref[g, :, (part * half + h) * D : (part * half + h + 1) * D] for h in range(half)], axis=0
                )
                s = lax.dot_general(q, keys, (((1,), (1,)), ((), ())), preferred_element_type=jnp.float32)
                s = jnp.where(live, s, NEG)
                old = mx[r, :]
                new = jnp.maximum(old, jnp.max(s, axis=1, keepdims=True))
                p = jnp.exp2(s * scale - (new * scale)[:, :1])
                factor = jnp.exp2((old - new) * scale)
                part_sum = p[:, :D]
                for i in range(1, NB // D):
                    part_sum = part_sum + p[:, i * D : (i + 1) * D]
                sm[r, :] = sm[r, :] * factor + part_sum
                mx[r, :] = new
                added = jnp.dot(p.astype(jnp.bfloat16), vals, preferred_element_type=jnp.float32)
                acc[r, :] = acc[r, :] * factor + added
            return 0

        lax.fori_loop(0, (count + NB - 1) // NB, block, 0)

        lane = lax.broadcasted_iota(jnp.int32, (tokens, D), 1)
        stats = jnp.zeros((tokens, D), jnp.float32)
        for h in range(heads):
            r = pl.ds(h * tokens, tokens)
            total = jnp.sum(sm[r, :], axis=1, keepdims=True)
            o_ref[g, :, h * D : (h + 1) * D] = (acc[r, :] / total).astype(jnp.bfloat16)
            lse = mx[r, :] * scale + jnp.log2(total)
            hi = lse.astype(jnp.bfloat16).astype(jnp.float32)
            mid = (lse - hi).astype(jnp.bfloat16).astype(jnp.float32)
            lo = lse - hi - mid
            stats = jnp.where(lane == h, hi, stats)
            stats = jnp.where(lane == heads + h, mid, stats)
            stats = jnp.where(lane == 2 * heads + h, lo, stats)
        o_ref[g, :, heads * D :] = stats.astype(jnp.bfloat16)
        return 0

    lax.fori_loop(0, TEAM, one_team, 0)


def combine_kernel(p_ref, o_ref):
    heads = o_ref.shape[1] // D
    stats = [p_ref[g, :, heads * D :].astype(jnp.float32) for g in range(TEAM)]
    for h in range(heads):
        lse = [
            s[:, h : h + 1] + s[:, heads + h : heads + h + 1] + s[:, 2 * heads + h : 2 * heads + h + 1] for s in stats
        ]
        top = functools.reduce(jnp.maximum, lse)
        w = [jnp.exp2(v - top) for v in lse]
        inv = 1.0 / functools.reduce(jnp.add, w)
        total = None
        for g in range(TEAM):
            term = p_ref[g, :, h * D : (h + 1) * D].astype(jnp.float32) * (w[g] * inv)
            total = term if total is None else total + term
        o_ref[:, h * D : (h + 1) * D] = total.astype(jnp.bfloat16)


VMEM = pl.BlockSpec(memory_space=pltpu.VMEM)
SMEM = pl.BlockSpec(memory_space=pltpu.SMEM)


def local(queries, keys, values, block_mask, lengths):
    groups = block_mask.shape[0]
    tokens, width = queries.shape
    heads = width // D
    x = lax.axis_index("x")
    rest = lax.axis_index(("yh", "z"))
    mine = keys.shape[0]
    kv_heads = keys.shape[1] // D
    both = jnp.stack([keys.reshape(mine // TEAM, TEAM, kv_heads, D), values.reshape(mine // TEAM, TEAM, kv_heads, D)], 3)
    both = both.transpose(1, 2, 0, 3, 4).reshape(TEAM, 1, kv_heads, mine // TEAM, 2 * D)
    both = jnp.broadcast_to(both, (TEAM, 4, kv_heads, mine // TEAM, 2 * D))
    both = both.reshape(TEAM * 4 * kv_heads, mine // TEAM, 2 * D)
    near = lax.all_to_all(both, ("x", "yh", "yl", "c"), split_axis=0, concat_axis=0, tiled=True)
    near = near.reshape(1, TEAM * 4 * PART, 2 * D)
    far = lax.all_to_all(
        jnp.broadcast_to(near, (8, TEAM * 4 * PART, 2 * D)), "z", split_axis=0, concat_axis=0, tiled=True
    )
    kv = far.reshape(groups * PART, 2 * D)
    team = lax.all_to_all(
        jnp.broadcast_to(queries[None], (TEAM, tokens, width)), "x", split_axis=0, concat_axis=0, tiled=True
    )
    me = jnp.stack([x, rest]).astype(jnp.int32)
    room = groups * PART + NB
    partial = pl.pallas_call(
        attend_kernel,
        out_shape=jax.ShapeDtypeStruct((TEAM, tokens, width + D), jnp.bfloat16),
        in_specs=[SMEM, SMEM, SMEM, VMEM, VMEM],
        out_specs=VMEM,
        scratch_shapes=[
            pltpu.VMEM((room, D), jnp.float32),
            pltpu.VMEM((room, D), jnp.float32),
            pltpu.VMEM((heads * tokens, D), jnp.float32),
            pltpu.VMEM((heads * tokens, D), jnp.float32),
            pltpu.VMEM((heads * tokens, D), jnp.float32),
        ],
        compiler_params=pltpu.CompilerParams(vmem_limit_bytes=40 * 2**20),
        name="attend",
    )(me, block_mask, lengths, team, kv)
    back = lax.all_to_all(partial, "x", split_axis=0, concat_axis=0, tiled=True)
    return pl.pallas_call(
        combine_kernel,
        out_shape=jax.ShapeDtypeStruct((tokens, width), jnp.bfloat16),
        in_specs=[VMEM],
        out_specs=VMEM,
        name="combine",
    )(back)


def solution(mesh):
    fine = Mesh(mesh.devices.reshape(4, 4, 8, 2, 2), ("x", "yh", "z", "yl", "c"))
    frames, heads = ("x", "yh", "z"), ("yl", "c")
    return jax.shard_map(
        local,
        mesh=fine,
        in_specs=(P(frames, heads), P(frames + heads, None), P(frames + heads, None), P(), P()),
        out_specs=P(frames, heads),
        check_vma=False,
    )
```

time: 410 us -> 156 us (0.38)
  the two profiles are of different devices: /device:TPU:126 before, /device:TPU:16 now
where the time goes in v1:
time: 156 us; the launch traced here: 155 us
  blocking collectives  60.3 us (39%)
  waiting for transfers between devices  50 us (32%)
  Pallas kernels  30.1 us (19%)
  starting transfers between devices  10.4 us (7%)
  local copies, waits for them, and re-layouts  4.12 us (3%)
    all_to_all x1, waiting for transfers between devices, local(): lax.all_to_all(jnp.broadcast_to(near, (8, TEAM * 4 * PART, 2 * D)), 'z',...  50 us
    pallas_call x1, Pallas kernels, local(): pl.pallas_call(attend_kernel, out_shape=jax.ShapeDtypeStruct((TEAM, token...  27.3 us
    all_to_all x1, blocking collectives, local(): lax.all_to_all(both, ('x', 'yh', 'yl', 'c'), split_axis=0, concat_axis=0,...  21.8 us
    all_to_all x1, blocking collectives, local(): back = lax.all_to_all(partial, 'x', split_axis=0, concat_axis=0, tiled=True)  20.1 us
    all_to_all x1, blocking collectives, local(): lax.all_to_all(jnp.broadcast_to(queries[None], (TEAM, tokens, width)), 'x...  18.4 us
    all_to_all x1, starting transfers between devices, local(): lax.all_to_all(jnp.broadcast_to(near, (8, TEAM * 4 * PART, 2 * D)), 'z',...  10.4 us
  transfers between devices with their start and end apart: 1, of which 1 were waited for; matrix products, arithmetic and copies ran while one was open for 0% of the time, Pallas kernels for 0%

profile of v1, /device:TPU:16, one launch (start us, length us, event | category | flops | bytes accessed | tf_op | source)
XLA Modules:
  0.0 155.1 jit_solution(7996823220910599204)
XLA Ops:
  0.0 0.8 stack_reshape.6
  0.8 0.8 stack_reshape.7
  1.7 21.8 %all_to_all.20 = bf16[64,8,256]{2,1,0:T(8,128)(2,1)S(1)} all-to-all(bf16[64,8,256]{2,1,0:T(8,128)(2,1)S(1)} %bitcast.12), channel_id=1, replica_groups=mesh['x'=4,'yh'=4,'z'=8,'yl'=2,'c'=2] {'x','yh','yl','c'}, dimensions={0} | all-to-all | bytes 524288 | tf_op jit(solution)/shard_map/all_to_all | solution.py:127
  23.5 1.1 broadcast_in_dim.20
  24.6 18.4 %all_to_all.21.q_ref = bf16[4,128,1024]{2,1,0:T(8,128)(2,1)S(1)} all-to-all(bf16[4,128,1024]{2,1,0:T(8,128)(2,1)S(1)} %broadcast_in_dim.20), channel_id=1, replica_groups=mesh['x'=4,'yh'=4,'z'=8,'yl'=2,'c'=2] {'x'}, dimensions={0} | all-to-all | bytes 2097152 | tf_op jit(solution)/shard_map/all_to_all | solution.py:133
  42.9 1.5 broadcast_in_dim.24
  44.4 0.0 copy-start
  44.4 0.0 copy-start.1
  44.4 10.4 %all-to-all-start.2 = ((bf16[8,512,256]{2,1,0:T(8,128)(2,1)}), bf16[8,512,256]{2,1,0:T(8,128)(2,1)S(1)}, u32[]{:S(2)}, u32[]{:S(2)}) async-start(bf16[8,512,256]{2,1,0:T(8,128)(2,1)} %broadcast_in_dim.24), calls=%async_computation.2 | async-start | bytes 4194304 | tf_op jit(solution)/shard_map/all_to_all | solution.py:129
  54.9 0.1 pad_add_fusion.me_ref
  54.9 50.0 %all-to-all-done.2 = bf16[8,512,256]{2,1,0:T(8,128)(2,1)S(1)} async-done(((bf16[8,512,256]{2,1,0:T(8,128)(2,1)}), bf16[8,512,256]{2,1,0:T(8,128)(2,1)S(1)}, u32[]{:S(2)}, u32[]{:S(2)}) %all-to-all-start.2) | async-done | bytes 2097184 | tf_op jit(solution)/shard_map/all_to_all | solution.py:129
  105.0 0.0 copy-done
  105.0 0.0 copy-done.1
  105.0 27.3 %attend.1 = bf16[4,128,1152]{2,1,0:T(8,128)(2,1)S(1)} custom-call(s32[2]{0:T(128)S(1)} %pad_add_fusion.me_ref, s32[128,128]{1,0:T(8,128)S(1)} %copy-done, s32[128]{0:T(128)S(1)} %copy-done.1, bf16[4,128,1024]{2,1,0:T(8,128)(2,1)S(1)} %all_to_all.21.q_ref, bf16[4096,256]{1,0:T(8,128)(2,1)S(1)} %bitcast.10), custom_call_target="tpu_custom_call" | custom-call | tf_op jit(solution)/shard_map/attend/pallas_call | solution.py:138
  132.3 20.1 %all_to_all.22.p_ref = bf16[4,128,1152]{2,1,0:T(8,128)(2,1)} all-to-all(bf16[4,128,1152]{2,1,0:T(8,128)(2,1)S(1)} %attend.1), channel_id=1, replica_groups=mesh['x'=4,'yh'=4,'z'=8,'yl'=2,'c'=2] {'x'}, dimensions={0} | all-to-all | bytes 2359296 | tf_op jit(solution)/shard_map/all_to_all | solution.py:153
  152.3 2.8 %combine.1 = bf16[128,1024]{1,0:T(8,128)(2,1)} custom-call(bf16[4,128,1152]{2,1,0:T(8,128)(2,1)} %all_to_all.22.p_ref), custom_call_target="tpu_custom_call" | custom-call | tf_op jit(solution)/shard_map/combine/pallas_call | solution.py:154
  (3 shorter events, 0.1 us)
Async XLA Ops:
  44.4 60.6 %copy-start = (s32[128,128]{1,0:T(8,128)S(1)}, s32[128,128]{1,0:T(8,128)}, u32[]{:S(2)}) copy-start(s32[128,128]{1,0:T(8,128)} %mask_ref.1) | copy-start | bytes 196612
  44.4 60.6 %copy-start.1 = (s32[128]{0:T(128)S(1)}, s32[128]{0:T(128)}, u32[]{:S(2)}) copy-start(s32[128]{0:T(128)} %len_ref.1) | copy-start | bytes 1540
  44.4 60.5 %all-to-all-start.2 = ((bf16[8,512,256]{2,1,0:T(8,128)(2,1)}), bf16[8,512,256]{2,1,0:T(8,128)(2,1)S(1)}, u32[]{:S(2)}, u32[]{:S(2)}) async-start(bf16[8,512,256]{2,1,0:T(8,128)(2,1)} %broadcast_in_dim.24), calls=%async_computation.2 | async-start | bytes 4194304 | tf_op jit(solution)/shard_map/all_to_all | solution.py:129

commit v2 on v1

v2 whole, which is shorter than its diff:
```python
import functools
import math

import jax
import jax.numpy as jnp
from jax import lax
from jax.experimental import pallas as pl
from jax.experimental.pallas import tpu as pltpu
from jax.sharding import Mesh, PartitionSpec as P


D = 128
LOG2E = math.log2(math.e)
NEG = -1e30
NB = 512
SIDE = 4
EXTRA = 16
TEAM = 4
PART = 32
VMEM = pl.BlockSpec(memory_space=pltpu.VMEM)
SMEM = pl.BlockSpec(memory_space=pltpu.SMEM)


def attend_kernel(pieces, first, last, *refs):
    me_ref, mask_ref, len_ref, q_ref = refs[:4]
    kv_refs = refs[4 : 4 + len(pieces)]
    refs = refs[4 + len(pieces) :]
    if not first:
        acc_in, mx_in, sm_in = refs[:3]
        refs = refs[3:]
    if last:
        o_ref, kf, vf, acc, mx, sm = refs
    else:
        acc_out, mx_out, sm_out, kf, vf, acc, mx, sm = refs
    groups = mask_ref.shape[0]
    per_x = groups // TEAM
    tokens = q_ref.shape[1]
    heads = q_ref.shape[2] // D
    x, rest, zb = me_ref[0], me_ref[1], me_ref[2]
    scale = D**-0.5 * LOG2E
    bias = TEAM - 1 - x
    span = SIDE * tokens

    counts = (jnp.int32(0),) * TEAM
    for kv_ref, (chunk0, chunks, shift) in zip(kv_refs, pieces):
        near = (zb + shift) & 3

        def pack(c, offs):
            j = ((c + chunk0) << 2) + near
            at = pl.multiple_of(c * PART, PART)
            key = kv_ref[pl.ds(at, PART), :D].astype(jnp.float32)
            val = kv_ref[pl.ds(at, PART), D:].astype(jnp.float32)
            live = lax.shift_right_logical(len_ref[j] + bias, 2)
            out = []
            for g in range(TEAM):
                kf[g, pl.ds(offs[g], PART), :] = key
                vf[g, pl.ds(offs[g], PART), :] = val
                out.append(offs[g] + jnp.where(mask_ref[g * per_x + rest, j] > 0, live, 0))
            return tuple(out)

        counts = lax.fori_loop(0, chunks, pack, counts, unroll=4)
    for g in range(TEAM):
        vf[g, pl.ds(counts[g], NB), :] = jnp.zeros((NB, D), jnp.float32)

    def one_team(g, _):
        count = counts[TEAM - 1]
        for i in range(TEAM - 1):
            count = jnp.where(g == i, counts[i], count)

        if first:
            acc[...] = jnp.zeros(acc.shape, jnp.float32)
            mx[...] = jnp.full(mx.shape, NEG, jnp.float32)
            sm[...] = jnp.zeros(sm.shape, jnp.float32)
        else:
            acc[...] = acc_in[g]
            mx[...] = mx_in[g]
            sm[...] = sm_in[g]

        def block(at, size, masked):
            keys = kf[g, pl.ds(at, size), :].astype(jnp.bfloat16)
            vals = vf[g, pl.ds(at, size), :].astype(jnp.bfloat16).T
            if masked:
                live = lax.broadcasted_iota(jnp.int32, (size, 1), 0) < count - at

            def scores(part):
                q = jnp.concatenate(
                    [q_ref[g, :, (part * SIDE + h) * D : (part * SIDE + h + 1) * D] for h in range(SIDE)], axis=0
                )
                s = lax.dot_general(keys, q, (((1,), (1,)), ((), ())), preferred_element_type=jnp.float32)
                return jnp.where(live, s, NEG) if masked else s

            parts = heads // SIDE
            ahead = scores(0)
            for part in range(parts):
                s = ahead
                if part + 1 < parts:
                    ahead = scores(part + 1)
                c = pl.ds(part * span, span)
                old = mx[:, c]
                new = jnp.maximum(old, jnp.max(s, axis=0, keepdims=True))
                p = jnp.exp2(s * scale - new * scale)
                factor = jnp.exp2((old - new) * scale)
                sm[:, c] = sm[:, c] * factor + jnp.sum(p, axis=0, keepdims=True)
                mx[:, c] = new
                added = jnp.dot(vals, p.astype(jnp.bfloat16), preferred_element_type=jnp.float32)
                acc[:, c] = acc[:, c] * factor + added

        full = lax.shift_right_logical(count, NB.bit_length() - 1)

        def full_block(b, _):
            block(pl.multiple_of(b * NB, NB), NB, False)
            return 0

        lax.fori_loop(0, full, full_block, 0)
        at = pl.multiple_of(full * NB, NB)

        @pl.when(count - at > NB // 2)
        def _():
            block(at, NB, True)

        @pl.when((count > at) & (count - at <= NB // 2))
        def _():
            block(at, NB // 2, True)

        if not last:
            acc_out[g] = acc[...]
            mx_out[g] = mx[...]
            sm_out[g] = sm[...]
            return 0

        total = sm[...]
        o_ref[g, :D, :] = (acc[...] * (1.0 / total)).astype(jnp.bfloat16)
        lse = mx[...] * scale + jnp.log2(total)
        hi = lse.astype(jnp.bfloat16).astype(jnp.float32)
        mid = (lse - hi).astype(jnp.bfloat16).astype(jnp.float32)
        lo = lse - hi - mid
        row = lax.broadcasted_iota(jnp.int32, (EXTRA, lse.shape[1]), 0)
        stats = jnp.where(row == 0, hi, jnp.where(row == 1, mid, jnp.where(row == 2, lo, 0.0)))
        o_ref[g, D:, :] = stats.astype(jnp.bfloat16)
        return 0

    lax.fori_loop(0, TEAM, one_team, 0)


def attend(me, block_mask, lengths, team, parts, state, last):
    tokens, width = team.shape[1:]
    rows = tokens * width // D
    pieces = tuple((chunk0, kv.shape[0] // PART, shift) for kv, chunk0, shift in parts)
    room = sum(kv.shape[0] for kv, _, _ in parts) + NB
    carried = [(D, rows), (1, rows), (1, rows)]
    if last:
        outs = jax.ShapeDtypeStruct((TEAM, D + EXTRA, rows), jnp.bfloat16)
    else:
        outs = [jax.ShapeDtypeStruct((TEAM,) + c, jnp.float32) for c in carried]
    operands = (me, block_mask, lengths, team) + tuple(kv for kv, _, _ in parts)
    aliases = {} if last else {len(operands) + i: i for i in range(len(state))}
    work = room * rows
    return pl.pallas_call(
        functools.partial(attend_kernel, pieces, not state, last),
        out_shape=outs,
        in_specs=[SMEM] * 3 + [VMEM] * (len(operands) - 3 + len(state)),
        out_specs=VMEM if last else [VMEM] * 3,
        scratch_shapes=[pltpu.VMEM((TEAM, room, D), jnp.float32)] * 2 + [pltpu.VMEM(c, jnp.float32) for c in carried],
        input_output_aliases=aliases,
        compiler_params=pltpu.CompilerParams(vmem_limit_bytes=32 * 2**20),
        cost_estimate=pl.CostEstimate(flops=8 * D * work, bytes_accessed=2**20, transcendentals=2 * work),
    )(*operands, *state)


def combine_kernel(p_ref, o_ref):
    heads = o_ref.shape[1] // D
    tokens = o_ref.shape[0]
    lse = [jnp.sum(p_ref[g, D:, :].astype(jnp.float32)[:8], axis=0, keepdims=True) for g in range(TEAM)]
    top = functools.reduce(jnp.maximum, lse)
    w = [jnp.exp2(v - top) for v in lse]
    inv = 1.0 / functools.reduce(jnp.add, w)
    w = [v * inv for v in w]
    for h in range(heads):
        c = slice(h * tokens, (h + 1) * tokens)
        total = functools.reduce(jnp.add, [p_ref[g, :D, c].astype(jnp.float32) * w[g][:, c] for g in range(TEAM)])
        o_ref[:, h * D : (h + 1) * D] = total.T.astype(jnp.bfloat16)


def stages(queries, keys, values, block_mask, lengths):
    tokens, width = queries.shape
    x = lax.axis_index("x")
    zb = lax.axis_index("zb")
    rest = lax.axis_index(("yh", "za", "zb"))
    mine = keys.shape[0]
    kv_heads = keys.shape[1] // D
    both = jnp.stack([keys.reshape(mine // TEAM, TEAM, kv_heads, D), values.reshape(mine // TEAM, TEAM, kv_heads, D)], 3)
    both = both.transpose(1, 2, 0, 3, 4).reshape(TEAM, 1, kv_heads, mine // TEAM, 2 * D)
    both = jnp.broadcast_to(both, (TEAM, 8, kv_heads, mine // TEAM, 2 * D))
    both = both.reshape(TEAM * 8 * kv_heads, mine // TEAM, 2 * D)
    own = lax.all_to_all(both, ("x", "yh", "za", "yl", "c"), split_axis=0, concat_axis=0, tiled=True)
    own = own.reshape(TEAM * 8 * PART, 2 * D)
    spread = jnp.broadcast_to(queries[None], (TEAM, tokens, width))
    team = lax.all_to_all(spread, "x", split_axis=0, concat_axis=0, tiled=True)
    up = [(i, (i + 1) % 8) for i in range(8)]
    down = [(i, (i + 7) % 8) for i in range(8)]
    half = own.shape[0] // 2
    below = lax.ppermute(own, ("za", "zb"), up)
    above = lax.ppermute(own, ("za", "zb"), down)
    far_a = lax.ppermute(above[:half], ("za", "zb"), down)
    far_b = lax.ppermute(below[half:], ("za", "zb"), up)
    me = jnp.stack([x, rest, zb]).astype(jnp.int32)
    common = (me, block_mask, lengths, team)
    state = attend(*common, [(own, 0, 0)], (), False)
    state = attend(*common, [(below, 0, 3), (above, 0, 1)], state, False)
    partial = attend(*common, [(far_a, 0, 2), (far_b, half // PART, 2)], state, True)
    back = lax.all_to_all(partial, "x", split_axis=0, concat_axis=0, tiled=True)
    return pl.pallas_call(
        combine_kernel,
        out_shape=jax.ShapeDtypeStruct((tokens, width), jnp.bfloat16),
        in_specs=[VMEM],
        out_specs=VMEM,
        name="combine",
    )(back)


def solution(mesh):
    fine = Mesh(mesh.devices.reshape(4, 4, 2, 4, 2, 2), ("x", "yh", "za", "zb", "yl", "c"))
    frames, heads = ("x", "yh", "za", "zb"), ("yl", "c")
    return jax.shard_map(
        stages,
        mesh=fine,
        in_specs=(P(frames, heads), P(frames + heads, None), P(frames + heads, None), P(), P()),
        out_specs=P(frames, heads),
        check_vma=False,
    )
```

time: 156 us -> 115 us (0.74)
  the two profiles are of different devices: /device:TPU:16 before, /device:TPU:208 now
where the time goes in v2:
time: 115 us; the launch traced here: 114 us
  blocking collectives  58.2 us (51%)
  Pallas kernels  24.2 us (21%)
  starting transfers between devices  17.6 us (15%)
  waiting for transfers between devices  10.6 us (9%)
  local copies, waits for them, and re-layouts  3.51 us (3%)
    all_to_all x1, blocking collectives, stages(): lax.all_to_all(both, ('x', 'yh', 'za', 'yl', 'c'), split_axis=0, concat_a...  37.5 us
    pallas_call x3, Pallas kernels, attend(): pl.pallas_call(functools.partial(attend_kernel, pieces, not state, last),...  21.9 us
    all_to_all x1, blocking collectives, stages(): back = lax.all_to_all(partial, 'x', split_axis=0, concat_axis=0, tiled=True)  20.7 us
    ppermute x1, waiting for transfers between devices, stages(): above = lax.ppermute(own, ('za', 'zb'), down)  10.6 us
    ppermute x1, starting transfers between devices, stages(): far_b = lax.ppermute(below[half:], ('za', 'zb'), up)  5.12 us
    ppermute x1, starting transfers between devices, stages(): below = lax.ppermute(own, ('za', 'zb'), up)  4.53 us
    all_to_all x1, starting transfers between devices, stages(): team = lax.all_to_all(spread, 'x', split_axis=0, concat_axis=0, tiled=True)  3.51 us
    ppermute x1, starting transfers between devices, stages(): above = lax.ppermute(own, ('za', 'zb'), down)  2.53 us
  transfers between devices with their start and end apart: 5, of which 1 were waited for; matrix products, arithmetic and copies ran while one was open for 1% of the time, Pallas kernels for 13%

profile of v2, /device:TPU:208, one launch (start us, length us, event | category | flops | bytes accessed | tf_op | source)
XLA Modules:
  0.0 114.4 jit_solution(2400100137178943335)
XLA Ops:
  0.0 0.8 stack_reshape.6
  0.8 0.8 stack_reshape.7
  1.7 0.1 broadcast_in_dim.15
  1.7 37.5 %all_to_all.15 = bf16[128,8,256]{2,1,0:T(8,128)(2,1)S(1)} all-to-all(bf16[128,8,256]{2,1,0:T(8,128)(2,1)S(1)} %bitcast.13), channel_id=1, replica_groups=mesh['x'=4,'yh'=4,'za'=2,'zb'=4,'yl'=2,'c'=2] {'x','yh','za','yl','c'}, dimensions={0} | all-to-all | bytes 1048576 | tf_op jit(solution)/shard_map/all_to_all | solution.py:195
  39.2 0.0 copy-done.2
  39.2 1.1 broadcast_in_dim.6
  40.3 3.5 %all-to-all-start = ((bf16[4,128,1024]{2,1,0:T(8,128)(2,1)}), bf16[4,128,1024]{2,1,0:T(8,128)(2,1)S(1)}, u32[]{:S(2)}, u32[]{:S(2)}) async-start(bf16[4,128,1024]{2,1,0:T(8,128)(2,1)} %broadcast_in_dim.6), calls=%async_computation | async-start | bytes 2097152 | tf_op jit(solution)/shard_map/all_to_all | solution.py:198
  43.9 2.5 %collective-permute-start = (bf16[1024,256]{1,0:T(8,128)(2,1)S(1)}, bf16[1024,256]{1,0:T(8,128)(2,1)S(1)}, u32[]{:S(2)}, u32[]{:S(2)}) collective-permute-start(bf16[1024,256]{1,0:T(8,128)(2,1)S(1)} %bitcast.10), channel_id=1, source_target_pairs={{0,28},{4,0},{8,4},{12,8},{16,12},{20,16},{24,20},{28,24},{1,29},{... | collective-permute-start | bytes 1572872 | tf_op jit(solution)/shard_map/ppermute | solution.py:203
  46.4 4.5 %collective-permute-start.2 = (bf16[1024,256]{1,0:T(8,128)(2,1)S(1)}, bf16[1024,256]{1,0:T(8,128)(2,1)S(1)}, u32[]{:S(2)}, u32[]{:S(2)}) collective-permute-start(bf16[1024,256]{1,0:T(8,128)(2,1)S(1)} %bitcast.11), channel_id=1, source_target_pairs={{0,4},{4,8},{8,12},{12,16},{16,20},{20,24},{24,28},{28,0},{1,5},{5... | collective-permute-start | bytes 1572872 | tf_op jit(solution)/shard_map/ppermute | solution.py:202
  50.9 0.1 pad_add_fusion.refs_0_
  51.0 10.6 %collective-permute-done.refs_5_ = bf16[1024,256]{1,0:T(8,128)(2,1)S(1)} collective-permute-done((bf16[1024,256]{1,0:T(8,128)(2,1)S(1)}, bf16[1024,256]{1,0:T(8,128)(2,1)S(1)}, u32[]{:S(2)}, u32[]{:S(2)}) %collective-permute-start) | collective-permute-done | bytes 524320 | tf_op jit(solution)/shard_map/ppermute | solution.py:203
  61.6 1.9 %collective-permute-start.1 = (bf16[512,256]{1,0:T(8,128)(2,1)S(1)}, bf16[512,256]{1,0:T(8,128)(2,1)S(1)}, u32[]{:S(2)}, u32[]{:S(2)}) collective-permute-start(bf16[512,256]{1,0:T(8,128)(2,1)S(1)} %slice.8), channel_id=1, source_target_pairs={{0,28},{4,0},{8,4},{12,8},{16,12},{20,16},{24,20},{28,24},{1,29},{... | collective-permute-start | bytes 786440 | tf_op jit(solution)/shard_map/ppermute | solution.py:204
  63.6 0.0 collective-permute-done.2.refs_4_
  63.6 0.7 slice.9
  64.3 5.1 %collective-permute-start.3 = (bf16[512,256]{1,0:T(8,128)(2,1)}, bf16[512,256]{1,0:T(8,128)(2,1)S(1)}, u32[]{:S(2)}, u32[]{:S(2)}) collective-permute-start(bf16[512,256]{1,0:T(8,128)(2,1)} %slice.9), channel_id=1, source_target_pairs={{0,4},{4,8},{8,12},{12,16},{16,20},{20,24},{24,28},{28,0},{1,5},{5... | collective-permute-start | bytes 786440 | tf_op jit(solution)/shard_map/ppermute | solution.py:205
  69.4 0.0 all-to-all-done.refs_3_
  69.4 0.0 copy-done
  69.5 6.3 %shard_map.55 = (f32[4,128,1024]{2,1,0:T(8,128)S(1)}, f32[4,1,1024]{2,1,0:T(1,128)S(1)}, f32[4,1,1024]{2,1,0:T(1,128)S(1)}) custom-call(s32[3]{0:T(128)S(1)} %pad_add_fusion.refs_0_, s32[128,128]{1,0:T(8,128)S(1)} %copy-done, s32[128]{0:T(128)S(1)} %copy-done.1, bf16[4,128,1024]{2,1,0:T(8,128)(2,1)S(1)} %all-to-all-done.refs_3_, bf16[1024,256]{1,0:T(8,128)(2,1)S(1)} %bitcast.12), custom_call_target="tpu_custom_call" | custom-call | flops 1610612736 | bytes 1048576 | tf_op jit(solution)/shard_map/pallas_call | solution.py:158
  75.8 9.1 %shard_map.56 = (f32[4,128,1024]{2,1,0:T(8,128)S(1)}, f32[4,1,1024]{2,1,0:T(1,128)S(1)}, f32[4,1,1024]{2,1,0:T(1,128)S(1)}) custom-call(s32[3]{0:T(128)S(1)} %pad_add_fusion.refs_0_, s32[128,128]{1,0:T(8,128)S(1)} %copy-done, s32[128]{0:T(128)S(1)} %copy-done.1, ...), custom_call_target="tpu_custom_call", output_to_operand_aliasing={{0}: (6, {}), {1}: (7, {}), {2}: (8, {})} | custom-call | flops 2684354560 | bytes 1048576 | tf_op jit(solution)/shard_map/pallas_call | solution.py:158
  84.9 0.0 collective-permute-done.1.refs_4_
  84.9 0.0 collective-permute-done.3.refs_5_
  84.9 6.4 %shard_map.57 = bf16[4,144,1024]{2,1,0:T(8,128)(2,1)S(1)} custom-call(s32[3]{0:T(128)S(1)} %pad_add_fusion.refs_0_, s32[128,128]{1,0:T(8,128)S(1)} %copy-done, s32[128]{0:T(128)S(1)} %copy-done.1, bf16[4,128,1024]{2,1,0:T(8,128)(2,1)S(1)} %all-to-all-done.refs_3_, bf16[512,256]{1,0:T(8,128)(2,1)S(1)} %collective-permute-done.1.refs_4_, ...), custom_call_target="tpu_custom_call" | custom-call | flops 1610612736 | bytes 1048576 | tf_op jit(solution)/shard_map/pallas_call | solution.py:158
  91.4 20.7 %all_to_all.16.p_ref = bf16[4,144,1024]{2,1,0:T(8,128)(2,1)} all-to-all(bf16[4,144,1024]{2,1,0:T(8,128)(2,1)S(1)} %shard_map.57), channel_id=1, replica_groups=mesh['x'=4,'yh'=4,'za'=2,'zb'=4,'yl'=2,'c'=2] {'x'}, dimensions={0} | all-to-all | bytes 2359296 | tf_op jit(solution)/shard_map/all_to_all | solution.py:211
  112.1 2.3 %combine.1 = bf16[128,1024]{1,0:T(8,128)(2,1)} custom-call(bf16[4,144,1024]{2,1,0:T(8,128)(2,1)} %all_to_all.16.p_ref), custom_call_target="tpu_custom_call" | custom-call | tf_op jit(solution)/shard_map/combine/pallas_call | solution.py:212
  (7 shorter events, 0.1 us)
Async XLA Ops:
  0.0 39.2 %copy-start.2 = (bf16[128,1024]{1,0:T(8,128)(2,1)S(1)}, bf16[128,1024]{1,0:T(8,128)(2,1)}, u32[]{:S(2)}) copy-start(bf16[128,1024]{1,0:T(8,128)(2,1)} %param.5) | copy-start | bytes 786436
  39.2 30.2 %copy-start = (s32[128,128]{1,0:T(8,128)S(1)}, s32[128,128]{1,0:T(8,128)}, u32[]{:S(2)}) copy-start(s32[128,128]{1,0:T(8,128)} %refs_1_.5) | copy-start | bytes 196612
  39.2 30.2 %copy-start.1 = (s32[128]{0:T(128)S(1)}, s32[128]{0:T(128)}, u32[]{:S(2)}) copy-start(s32[128]{0:T(128)} %refs_2_.5) | copy-start | bytes 1540
  40.3 29.1 %all-to-all-start = ((bf16[4,128,1024]{2,1,0:T(8,128)(2,1)}), bf16[4,128,1024]{2,1,0:T(8,128)(2,1)S(1)}, u32[]{:S(2)}, u32[]{:S(2)}) async-start(bf16[4,128,1024]{2,1,0:T(8,128)(2,1)} %broadcast_in_dim.6), calls=%async_computation | async-start | bytes 2097152 | tf_op jit(solution)/shard_map/all_to_all | solution.py:198
  43.9 17.8 %collective-permute-start = (bf16[1024,256]{1,0:T(8,128)(2,1)S(1)}, bf16[1024,256]{1,0:T(8,128)(2,1)S(1)}, u32[]{:S(2)}, u32[]{:S(2)}) collective-permute-start(bf16[1024,256]{1,0:T(8,128)(2,1)S(1)} %bitcast.10), channel_id=1, source_target_pairs={{0,28},{4,0},{8,4},{12,8},{16,12},{20,16},{24,20},{28,24},{1,29},{... | collective-permute-start | bytes 1572872 | tf_op jit(solution)/shard_map/ppermute | solution.py:203
  46.4 17.2 %collective-permute-start.2 = (bf16[1024,256]{1,0:T(8,128)(2,1)S(1)}, bf16[1024,256]{1,0:T(8,128)(2,1)S(1)}, u32[]{:S(2)}, u32[]{:S(2)}) collective-permute-start(bf16[1024,256]{1,0:T(8,128)(2,1)S(1)} %bitcast.11), channel_id=1, source_target_pairs={{0,4},{4,8},{8,12},{12,16},{16,20},{20,24},{24,28},{28,0},{1,5},{5... | collective-permute-start | bytes 1572872 | tf_op jit(solution)/shard_map/ppermute | solution.py:202
  61.6 23.3 %collective-permute-start.1 = (bf16[512,256]{1,0:T(8,128)(2,1)S(1)}, bf16[512,256]{1,0:T(8,128)(2,1)S(1)}, u32[]{:S(2)}, u32[]{:S(2)}) collective-permute-start(bf16[512,256]{1,0:T(8,128)(2,1)S(1)} %slice.8), channel_id=1, source_target_pairs={{0,28},{4,0},{8,4},{12,8},{16,12},{20,16},{24,20},{28,24},{1,29},{... | collective-permute-start | bytes 786440 | tf_op jit(solution)/shard_map/ppermute | solution.py:204
  64.3 20.6 %collective-permute-start.3 = (bf16[512,256]{1,0:T(8,128)(2,1)}, bf16[512,256]{1,0:T(8,128)(2,1)S(1)}, u32[]{:S(2)}, u32[]{:S(2)}) collective-permute-start(bf16[512,256]{1,0:T(8,128)(2,1)} %slice.9), channel_id=1, source_target_pairs={{0,4},{4,8},{8,12},{12,16},{16,20},{20,24},{24,28},{28,0},{1,5},{5... | collective-permute-start | bytes 786440 | tf_op jit(solution)/shard_map/ppermute | solution.py:205
